TPU v7x, 32 devices: a whole 2x2x4 slice. The times are simulated.
32 devices in a mesh: row: 8 (over y, x, core), col: 4 (over z).
Axes of the slice: x: 2, y: 2, z: 4, core: 2. Of those that a mesh axis runs over, the one named last changes fastest.
Arguments:
- blocks: bfloat16 [8, 4, 368, 128, 128], P('row', 'col'), may hold values from -0.125 to 0.125
- block_rows: int32 [8, 4, 368], P('row', 'col'), may hold values from 0 to 31, as said below
- block_cols: int32 [8, 4, 368], P('row', 'col'), may hold values from 0 to 63
- counts: int32 [8, 4], P('row', 'col'), may hold values from 1 to 368, as said below
- features: bfloat16 [32768, 256], P(('col', 'row')), may hold values from -6 to 6
Outputs:
- aggregated: bfloat16 [32768, 256], P(('row', 'col'))
Inputs may be any that keep to these rules, and one draw needn't show every extreme that they name: `block_rows`: within one tile the live slots name distinct pairs of block row and block column. `counts`: some tile holds exactly 368 live blocks in every draw.
All inputs are finite; a program needn't handle non-finite values.
Results may differ from a plain program's by a relative error of at most 0.013.
Values may be sent and summed in bfloat16 or wider, within the bound.
A program may use at most 128 MiB of HBM per device.

v0:
```python
import jax
import jax.numpy as jnp
from jax import lax
from jax.sharding import PartitionSpec as P


def on_device(blocks, block_rows, block_cols, counts, features):
    feature_width = features.shape[1]
    block_size = blocks.shape[-1]
    max_blocks = blocks.shape[2]
    group_size = max_blocks // 8
    row_blocks = lax.axis_size("col") * (features.shape[0] // block_size)
    panel_rows = lax.all_gather(features, "row", axis=0, tiled=True)
    panel_blocks = panel_rows.reshape(-1, block_size, feature_width)
    tile_blocks = blocks[0, 0]
    tile_rows = block_rows[0, 0]
    tile_cols = block_cols[0, 0]
    live_count = counts[0, 0]

    def accumulate(group_index, running):
        first_slot = group_index * group_size
        weights = lax.dynamic_slice_in_dim(tile_blocks, first_slot, group_size, 0)
        rows_slice = lax.dynamic_slice_in_dim(tile_rows, first_slot, group_size, 0)
        cols_slice = lax.dynamic_slice_in_dim(tile_cols, first_slot, group_size, 0)
        positions = first_slot + jnp.arange(group_size, dtype=jnp.int32)
        weights = jnp.where(
            (positions < live_count)[:, None, None], weights, jnp.zeros_like(weights)
        )
        gathered = panel_blocks[cols_slice, :, 0:feature_width]
        product = jnp.einsum("gik,gkf->gif", weights, gathered, preferred_element_type=jnp.float32)
        return running.at[rows_slice].add(product)

    initial = jnp.zeros((row_blocks, block_size, feature_width - 0), jnp.float32)
    groups = 8
    running = lax.fori_loop(0, groups, accumulate, initial)
    return lax.psum_scatter(
        running.reshape(row_blocks * block_size, feature_width - 0).astype(jnp.bfloat16),
        "col",
        scatter_dimension=0,
        tiled=True,
    )


def solution(mesh):
    return jax.shard_map(
        on_device,
        mesh=mesh,
        in_specs=(
            P("row", "col", None, None, None),
            P("row", "col", None),
            P("row", "col", None),
            P("row", "col"),
            P(("col", "row"), None),
        ),
        out_specs=P(("row", "col"), None),
        check_vma=False,
    )
```

profile of v0, /device:TPU:0, one launch (start us, length us, event | category | flops | bytes accessed | tf_op | source)
XLA Modules:
  0.0 290.6 jit_solution(15859293063505907300)
XLA Ops:
  6.5 0.7 all-gather.2.cloned.1.call-update
  7.3 0.7 reduce
  8.0 0.7 reduce.1
  8.7 39.9 %all-gather.2.cloned.1.call-done = bf16[8192,256]{1,0:T(8,128)(2,1)} async-done(((bf16[1024,256]{1,0:T(8,128)(2,1)}), bf16[8192,256]{1,0:T(8,128)(2,1)}) %all-gather.2.cloned.1.call-update) | async-done | bytes 4194320 | tf_op jit(solution)/shard_map/all_gather | solution.py:13
  48.6 2.6 broadcast_in_dim.38
  51.1 185.2 %while.13 = (s32[]{:T(128)}, f32[32,128,256]{2,1,0:T(8,128)}, s32[368]{0:T(512)S(1)}, s32[]{:T(128)}, bf16[368,128,128]{2,1,0:T(8,128)(2,1)}, /*index=5*/s32[368...) while((s32[]{:T(128)}, f32[32,128,256]{2,1,0:T(8,128)}, ...), condition=%wide.region_2.3_spmd, body=%wide.region_0.2_spmd.sunk | while | flops 388138368 | bytes 34674192 | solution.py:35
  51.1 0.7 add_compare_fusion.2
  51.8 0.1 compare_select_fusion.3
  51.9 2.9 %gather_fusion = bf16[46,128,256]{2,1,0:T(8,128)(2,1)S(1)} fusion(bf16[64,128,256]{2,1,0:T(8,128)(2,1)} %get-tuple-element.221, s32[1024]{0:T(1024)S(1)} %pad_clamp_fusion.2), kind=kCustom, calls=%fused_computation.clone.1 | custom fusion | bytes 6029496 | tf_op jit(solution)/shard_map/while/body/eval_jaxpr/gather | solution.py:29
  54.8 5.0 %fusion.13 = f32[46,128,256]{2,1,0:T(8,128)} fusion(bf16[46,128,256]{2,1,0:T(8,128)(2,1)S(1)} %gather_fusion, bf16[368,128,128]{2,1,0:T(8,128)(2,1)} %get-tuple-element.219, s32[]{:T(128)S(6)} %select_n.40, pred[46]{0:T(512)(128)(4,1)S(1)} %add_compare_fusion.2), kind=kOutput, calls=%fused_computation.2.clone.1 | convolution fusion | flops 386629632 | bytes 10551346 | tf_op jit(solution)/shard_map/while/body/eval_jaxpr/gik,gkf->gif/dot_general | solution.py:30
  59.8 14.4 %scatter_fusion = f32[32,128,256]{2,1,0:T(8,128)} fusion(f32[32,128,256]{2,1,0:T(8,128)} %get-tuple-element.205, s32[46]{0:T(128)S(1)} %get-tuple-element.191, f32[46,128,256]{2,1,0:T(8,128)} %fusion.13), kind=kCustom, calls=%fused_computation.1.clone.1 | custom fusion | flops 1507328 | bytes 18088120 | tf_op jit(solution)/shard_map/while/body/eval_jaxpr/scatter-add | solution.py:31
  74.1 0.7 add_compare_fusion.2
  74.8 0.1 compare_select_fusion.3
  74.9 2.9 %gather_fusion = bf16[46,128,256]{2,1,0:T(8,128)(2,1)S(1)} fusion(bf16[64,128,256]{2,1,0:T(8,128)(2,1)} %get-tuple-element.221, s32[1024]{0:T(1024)S(1)} %pad_clamp_fusion.2), kind=kCustom, calls=%fused_computation.clone.1 | custom fusion | bytes 6029496 | tf_op jit(solution)/shard_map/while/body/eval_jaxpr/gather | solution.py:29
  77.8 5.0 %fusion.13 = f32[46,128,256]{2,1,0:T(8,128)} fusion(bf16[46,128,256]{2,1,0:T(8,128)(2,1)S(1)} %gather_fusion, bf16[368,128,128]{2,1,0:T(8,128)(2,1)} %get-tuple-element.219, s32[]{:T(128)S(6)} %select_n.40, pred[46]{0:T(512)(128)(4,1)S(1)} %add_compare_fusion.2), kind=kOutput, calls=%fused_computation.2.clone.1 | convolution fusion | flops 386629632 | bytes 10551346 | tf_op jit(solution)/shard_map/while/body/eval_jaxpr/gik,gkf->gif/dot_general | solution.py:30
  82.8 14.5 %scatter_fusion = f32[32,128,256]{2,1,0:T(8,128)} fusion(f32[32,128,256]{2,1,0:T(8,128)} %get-tuple-element.205, s32[46]{0:T(128)S(1)} %get-tuple-element.191, f32[46,128,256]{2,1,0:T(8,128)} %fusion.13), kind=kCustom, calls=%fused_computation.1.clone.1 | custom fusion | flops 1507328 | bytes 18088120 | tf_op jit(solution)/shard_map/while/body/eval_jaxpr/scatter-add | solution.py:31
  97.2 0.7 add_compare_fusion.2
  97.9 0.1 compare_select_fusion.3
  98.0 2.9 %gather_fusion = bf16[46,128,256]{2,1,0:T(8,128)(2,1)S(1)} fusion(bf16[64,128,256]{2,1,0:T(8,128)(2,1)} %get-tuple-element.221, s32[1024]{0:T(1024)S(1)} %pad_clamp_fusion.2), kind=kCustom, calls=%fused_computation.clone.1 | custom fusion | bytes 6029496 | tf_op jit(solution)/shard_map/while/body/eval_jaxpr/gather | solution.py:29
  100.9 5.0 %fusion.13 = f32[46,128,256]{2,1,0:T(8,128)} fusion(bf16[46,128,256]{2,1,0:T(8,128)(2,1)S(1)} %gather_fusion, bf16[368,128,128]{2,1,0:T(8,128)(2,1)} %get-tuple-element.219, s32[]{:T(128)S(6)} %select_n.40, pred[46]{0:T(512)(128)(4,1)S(1)} %add_compare_fusion.2), kind=kOutput, calls=%fused_computation.2.clone.1 | convolution fusion | flops 386629632 | bytes 10551346 | tf_op jit(solution)/shard_map/while/body/eval_jaxpr/gik,gkf->gif/dot_general | solution.py:30
  105.9 14.5 %scatter_fusion = f32[32,128,256]{2,1,0:T(8,128)} fusion(f32[32,128,256]{2,1,0:T(8,128)} %get-tuple-element.205, s32[46]{0:T(128)S(1)} %get-tuple-element.191, f32[46,128,256]{2,1,0:T(8,128)} %fusion.13), kind=kCustom, calls=%fused_computation.1.clone.1 | custom fusion | flops 1507328 | bytes 18088120 | tf_op jit(solution)/shard_map/while/body/eval_jaxpr/scatter-add | solution.py:31
  120.4 0.7 add_compare_fusion.2
  121.0 0.1 compare_select_fusion.3
  121.1 2.9 %gather_fusion = bf16[46,128,256]{2,1,0:T(8,128)(2,1)S(1)} fusion(bf16[64,128,256]{2,1,0:T(8,128)(2,1)} %get-tuple-element.221, s32[1024]{0:T(1024)S(1)} %pad_clamp_fusion.2), kind=kCustom, calls=%fused_computation.clone.1 | custom fusion | bytes 6029496 | tf_op jit(solution)/shard_map/while/body/eval_jaxpr/gather | solution.py:29
  124.0 5.0 %fusion.13 = f32[46,128,256]{2,1,0:T(8,128)} fusion(bf16[46,128,256]{2,1,0:T(8,128)(2,1)S(1)} %gather_fusion, bf16[368,128,128]{2,1,0:T(8,128)(2,1)} %get-tuple-element.219, s32[]{:T(128)S(6)} %select_n.40, pred[46]{0:T(512)(128)(4,1)S(1)} %add_compare_fusion.2), kind=kOutput, calls=%fused_computation.2.clone.1 | convolution fusion | flops 386629632 | bytes 10551346 | tf_op jit(solution)/shard_map/while/body/eval_jaxpr/gik,gkf->gif/dot_general | solution.py:30
  129.0 14.3 %scatter_fusion = f32[32,128,256]{2,1,0:T(8,128)} fusion(f32[32,128,256]{2,1,0:T(8,128)} %get-tuple-element.205, s32[46]{0:T(128)S(1)} %get-tuple-element.191, f32[46,128,256]{2,1,0:T(8,128)} %fusion.13), kind=kCustom, calls=%fused_computation.1.clone.1 | custom fusion | flops 1507328 | bytes 18088120 | tf_op jit(solution)/shard_map/while/body/eval_jaxpr/scatter-add | solution.py:31
  143.3 0.7 add_compare_fusion.2
  143.9 0.1 compare_select_fusion.3
  144.0 2.9 %gather_fusion = bf16[46,128,256]{2,1,0:T(8,128)(2,1)S(1)} fusion(bf16[64,128,256]{2,1,0:T(8,128)(2,1)} %get-tuple-element.221, s32[1024]{0:T(1024)S(1)} %pad_clamp_fusion.2), kind=kCustom, calls=%fused_computation.clone.1 | custom fusion | bytes 6029496 | tf_op jit(solution)/shard_map/while/body/eval_jaxpr/gather | solution.py:29
  147.0 5.0 %fusion.13 = f32[46,128,256]{2,1,0:T(8,128)} fusion(bf16[46,128,256]{2,1,0:T(8,128)(2,1)S(1)} %gather_fusion, bf16[368,128,128]{2,1,0:T(8,128)(2,1)} %get-tuple-element.219, s32[]{:T(128)S(6)} %select_n.40, pred[46]{0:T(512)(128)(4,1)S(1)} %add_compare_fusion.2), kind=kOutput, calls=%fused_computation.2.clone.1 | convolution fusion | flops 386629632 | bytes 10551346 | tf_op jit(solution)/shard_map/while/body/eval_jaxpr/gik,gkf->gif/dot_general | solution.py:30
  151.9 14.6 %scatter_fusion = f32[32,128,256]{2,1,0:T(8,128)} fusion(f32[32,128,256]{2,1,0:T(8,128)} %get-tuple-element.205, s32[46]{0:T(128)S(1)} %get-tuple-element.191, f32[46,128,256]{2,1,0:T(8,128)} %fusion.13), kind=kCustom, calls=%fused_computation.1.clone.1 | custom fusion | flops 1507328 | bytes 18088120 | tf_op jit(solution)/shard_map/while/body/eval_jaxpr/scatter-add | solution.py:31
  166.5 0.7 add_compare_fusion.2
  167.2 0.1 compare_select_fusion.3
  167.3 2.9 %gather_fusion = bf16[46,128,256]{2,1,0:T(8,128)(2,1)S(1)} fusion(bf16[64,128,256]{2,1,0:T(8,128)(2,1)} %get-tuple-element.221, s32[1024]{0:T(1024)S(1)} %pad_clamp_fusion.2), kind=kCustom, calls=%fused_computation.clone.1 | custom fusion | bytes 6029496 | tf_op jit(solution)/shard_map/while/body/eval_jaxpr/gather | solution.py:29
  170.2 5.0 %fusion.13 = f32[46,128,256]{2,1,0:T(8,128)} fusion(bf16[46,128,256]{2,1,0:T(8,128)(2,1)S(1)} %gather_fusion, bf16[368,128,128]{2,1,0:T(8,128)(2,1)} %get-tuple-element.219, s32[]{:T(128)S(6)} %select_n.40, pred[46]{0:T(512)(128)(4,1)S(1)} %add_compare_fusion.2), kind=kOutput, calls=%fused_computation.2.clone.1 | convolution fusion | flops 386629632 | bytes 10551346 | tf_op jit(solution)/shard_map/while/body/eval_jaxpr/gik,gkf->gif/dot_general | solution.py:30
  175.2 14.6 %scatter_fusion = f32[32,128,256]{2,1,0:T(8,128)} fusion(f32[32,128,256]{2,1,0:T(8,128)} %get-tuple-element.205, s32[46]{0:T(128)S(1)} %get-tuple-element.191, f32[46,128,256]{2,1,0:T(8,128)} %fusion.13), kind=kCustom, calls=%fused_computation.1.clone.1 | custom fusion | flops 1507328 | bytes 18088120 | tf_op jit(solution)/shard_map/while/body/eval_jaxpr/scatter-add | solution.py:31
  189.8 0.7 add_compare_fusion.2
  190.5 0.1 compare_select_fusion.3
  190.6 2.9 %gather_fusion = bf16[46,128,256]{2,1,0:T(8,128)(2,1)S(1)} fusion(bf16[64,128,256]{2,1,0:T(8,128)(2,1)} %get-tuple-element.221, s32[1024]{0:T(1024)S(1)} %pad_clamp_fusion.2), kind=kCustom, calls=%fused_computation.clone.1 | custom fusion | bytes 6029496 | tf_op jit(solution)/shard_map/while/body/eval_jaxpr/gather | solution.py:29
  193.5 5.0 %fusion.13 = f32[46,128,256]{2,1,0:T(8,128)} fusion(bf16[46,128,256]{2,1,0:T(8,128)(2,1)S(1)} %gather_fusion, bf16[368,128,128]{2,1,0:T(8,128)(2,1)} %get-tuple-element.219, s32[]{:T(128)S(6)} %select_n.40, pred[46]{0:T(512)(128)(4,1)S(1)} %add_compare_fusion.2), kind=kOutput, calls=%fused_computation.2.clone.1 | convolution fusion | flops 386629632 | bytes 10551346 | tf_op jit(solution)/shard_map/while/body/eval_jaxpr/gik,gkf->gif/dot_general | solution.py:30
  198.5 14.6 %scatter_fusion = f32[32,128,256]{2,1,0:T(8,128)} fusion(f32[32,128,256]{2,1,0:T(8,128)} %get-tuple-element.205, s32[46]{0:T(128)S(1)} %get-tuple-element.191, f32[46,128,256]{2,1,0:T(8,128)} %fusion.13), kind=kCustom, calls=%fused_computation.1.clone.1 | custom fusion | flops 1507328 | bytes 18088120 | tf_op jit(solution)/shard_map/while/body/eval_jaxpr/scatter-add | solution.py:31
  213.1 0.7 add_compare_fusion.2
  213.8 0.1 compare_select_fusion.3
  213.8 2.9 %gather_fusion = bf16[46,128,256]{2,1,0:T(8,128)(2,1)S(1)} fusion(bf16[64,128,256]{2,1,0:T(8,128)(2,1)} %get-tuple-element.221, s32[1024]{0:T(1024)S(1)} %pad_clamp_fusion.2), kind=kCustom, calls=%fused_computation.clone.1 | custom fusion | bytes 6029496 | tf_op jit(solution)/shard_map/while/body/eval_jaxpr/gather | solution.py:29
  216.8 5.0 %fusion.13 = f32[46,128,256]{2,1,0:T(8,128)} fusion(bf16[46,128,256]{2,1,0:T(8,128)(2,1)S(1)} %gather_fusion, bf16[368,128,128]{2,1,0:T(8,128)(2,1)} %get-tuple-element.219, s32[]{:T(128)S(6)} %select_n.40, pred[46]{0:T(512)(128)(4,1)S(1)} %add_compare_fusion.2), kind=kOutput, calls=%fused_computation.2.clone.1 | convolution fusion | flops 386629632 | bytes 10551346 | tf_op jit(solution)/shard_map/while/body/eval_jaxpr/gik,gkf->gif/dot_general | solution.py:30
  221.7 14.6 %scatter_fusion = f32[32,128,256]{2,1,0:T(8,128)} fusion(f32[32,128,256]{2,1,0:T(8,128)} %get-tuple-element.205, s32[46]{0:T(128)S(1)} %get-tuple-element.191, f32[46,128,256]{2,1,0:T(8,128)} %fusion.13), kind=kCustom, calls=%fused_computation.1.clone.1 | custom fusion | flops 1507328 | bytes 18088120 | tf_op jit(solution)/shard_map/while/body/eval_jaxpr/scatter-add | solution.py:31
  236.3 3.8 %convert_element_type.6 = bf16[32,128,256]{2,1,0:T(8,128)(2,1)} convert(f32[32,128,256]{2,1,0:T(8,128)} %get-tuple-element.129) | non-fusion elementwise | flops 1048576 | bytes 6291456 | tf_op jit(solution)/shard_map/convert_element_type | solution.py:37
  240.1 43.6 %reduce-scatter.2.cloned.1.call-done = bf16[1024,256]{1,0:T(8,128)(2,1)} async-done(((bf16[4096,256]{1,0:T(8,128)(2,1)}), bf16[1024,256]{1,0:T(8,128)(2,1)}) %reduce-scatter.2.cloned.1.call-update) | async-done | bytes 524304 | tf_op jit(solution)/shard_map/reduce_scatter | solution.py:36
  (11 shorter events, 0.1 us)
Async XLA Ops:
  6.5 42.0 %all-gather.2.cloned.1.call-start = ((), (), s32[]{:S(2)}) async-start(), calls=%async_computation.1 | async-start | bytes 4718592 | tf_op jit(solution)/shard_map/all_gather | solution.py:13
  7.3 276.5 %reduce-scatter.2.cloned.1.call-start = ((), (), s32[]{:S(2)}) async-start(), calls=%async_computation.2 | async-start | bytes 2621440 | tf_op jit(solution)/shard_map/reduce_scatter | solution.py:36
Sparse Core Ops, SparseCore 0:
  9.2 39.2 all-gather.1
  240.3 43.4 reduce-scatter.1
where the time goes:
time: 292 us; the launch traced here: 291 us
  other arithmetic  127 us (43%)
  waiting for transfers between devices  84.2 us (29%)
  matrix products  39.7 us (14%)
  local copies, waits for them, and re-layouts  26 us (9%)
  between operations  13.4 us (5%)
    scatter-add x8, other arithmetic, accumulate(): return running.at[rows_slice].add(product)  116 us
    reduce_scatter x1, waiting for transfers between devices, on_device(): lax.psum_scatter(running.reshape(row_blocks * block_size, feature_width -...  43.6 us
    all_gather x1, waiting for transfers between devices, on_device(): panel_rows = lax.all_gather(features, 'row', axis=0, tiled=True)  39.9 us
    dot_general x8, matrix products, accumulate(): jnp.einsum('gik,gkf->gif', weights, gathered, preferred_element_type=jnp....  39.7 us
    gather x8, local copies, waits for them, and re-layouts, accumulate(): gathered = panel_blocks[cols_slice, :, 0:feature_width]  23.4 us
  transfers between devices with their start and end apart: 2, of which 2 were waited for; matrix products, arithmetic and copies ran while one was open for 0% of the time, Pallas kernels for 0%

commit v1 on v0

--- a/solution.py
+++ b/solution.py
@@ -2,6 +2,7 @@
 import jax.numpy as jnp
 from jax import lax
 from jax.sharding import PartitionSpec as P
+from jax.lax import all_to_all, axis_size
 
 
 def on_device(blocks, block_rows, block_cols, counts, features):
@@ -10,7 +11,12 @@
     max_blocks = blocks.shape[2]
     group_size = max_blocks // 8
     row_blocks = lax.axis_size("col") * (features.shape[0] // block_size)
-    panel_rows = lax.all_gather(features, "row", axis=0, tiled=True)
+    in_order = []
+    for _ in range(axis_size("row")):
+        in_order.append(features)
+    panel_rows = jnp.concatenate(
+        all_to_all(jnp.stack(in_order), axis_name="row", concat_axis=0, split_axis=0), axis=0
+    )
     panel_blocks = panel_rows.reshape(-1, block_size, feature_width)
     tile_blocks = blocks[0, 0]
     tile_rows = block_rows[0, 0]

time: 292 us -> 308 us (1.055)
  waiting for transfers between devices: 84.2 us -> 92.7 us
  starting transfers between devices: 0.04 us -> 5.37 us
  local copies, waits for them, and re-layouts: 26 us -> 29.2 us
    all_to_all x0 -> x1, waiting for transfers between devices: none -> 49.1 us  [on_device(): all_to_all(jnp.stack(in_order), axis_name='row', concat_axis=0, split_axi...]
    all_gather x1 -> x0, waiting for transfers between devices: 39.9 us -> none  [on_device(): panel_rows = lax.all_gather(features, 'row', axis=0, tiled=True)]
    all_to_all x0 -> x1, starting transfers between devices: none -> 5.33 us  [on_device(): all_to_all(jnp.stack(in_order), axis_name='row', concat_axis=0, split_axi...]
    another operation x0 -> x1, local copies, waits for them, and re-layouts: none -> 3.24 us  [on_device(): jnp.stack(in_order)]
where the time goes in v1:
time: 308 us; the launch traced here: 306 us
  other arithmetic  126 us (41%)
  waiting for transfers between devices  92.7 us (30%)
  matrix products  39.7 us (13%)
  local copies, waits for them, and re-layouts  29.2 us (9%)
  between operations  13.4 us (4%)
  starting transfers between devices  5.37 us (2%)
    scatter-add x8, other arithmetic, accumulate(): return running.at[rows_slice].add(product)  116 us
    all_to_all x1, waiting for transfers between devices, on_device(): all_to_all(jnp.stack(in_order), axis_name='row', concat_axis=0, split_axi...  49.1 us
    reduce_scatter x1, waiting for transfers between devices, on_device(): lax.psum_scatter(running.reshape(row_blocks * block_size, feature_width -...  43.6 us
    dot_general x8, matrix products, accumulate(): jnp.einsum('gik,gkf->gif', weights, gathered, preferred_element_type=jnp....  39.7 us
    gather x8, local copies, waits for them, and re-layouts, accumulate(): gathered = panel_blocks[cols_slice, :, 0:feature_width]  23.4 us
  transfers between devices with their start and end apart: 2, of which 2 were waited for; matrix products, arithmetic and copies ran while one was open for 0% of the time, Pallas kernels for 0%

profile of v1, /device:TPU:0, one launch (start us, length us, event | category | flops | bytes accessed | tf_op | source)
XLA Modules:
  0.0 306.4 jit_solution(10011990817115027331)
XLA Ops:
  6.5 3.2 %stack.2 = bf16[8,1024,256]{2,1,0:T(8,128)(2,1)} broadcast(bf16[1024,256]{1,0:T(8,128)(2,1)} %param.11), dimensions={1,2} | broadcast | bytes 4718592 | tf_op jit(solution)/shard_map/stack | solution.py:18
  9.8 5.3 %all-to-all-start = ((bf16[8,1024,256]{2,1,0:T(8,128)(2,1)}), bf16[8,1024,256]{2,1,0:T(8,128)(2,1)}, u32[]{:S(2)}, u32[]{:S(2)}) async-start(bf16[8,1024,256]{2,1,0:T(8,128)(2,1)} %stack.2), calls=%async_computation | async-start | bytes 8388608 | tf_op jit(solution)/shard_map/all_to_all | solution.py:18
  15.1 0.0 reduce-scatter.2.cloned.1.call-start
  15.2 49.1 %all-to-all-done = bf16[8,1024,256]{2,1,0:T(8,128)(2,1)} async-done(((bf16[8,1024,256]{2,1,0:T(8,128)(2,1)}), bf16[8,1024,256]{2,1,0:T(8,128)(2,1)}, u32[]{:S(2)}, u32[]{:S(2)}) %all-to-all-start) | async-done | bytes 4194336 | tf_op jit(solution)/shard_map/all_to_all | solution.py:18
  64.3 2.6 broadcast_in_dim.38
  66.9 185.2 %while.13 = (s32[]{:T(128)}, f32[32,128,256]{2,1,0:T(8,128)}, s32[368]{0:T(512)S(1)}, s32[]{:T(128)}, bf16[368,128,128]{2,1,0:T(8,128)(2,1)}, /*index=5*/s32[368...) while((s32[]{:T(128)}, f32[32,128,256]{2,1,0:T(8,128)}, ...), condition=%wide.region_2.3_spmd, body=%wide.region_0.2_spmd.sunk | while | flops 388138368 | bytes 34674192 | solution.py:41
  66.9 0.7 add_compare_fusion.2
  67.5 0.1 compare_select_fusion.3
  67.6 2.9 gather_fusion
  70.5 5.0 %fusion.13 = f32[46,128,256]{2,1,0:T(8,128)} fusion(bf16[46,128,256]{2,1,0:T(8,128)(2,1)S(1)} %gather_fusion, bf16[368,128,128]{2,1,0:T(8,128)(2,1)} %get-tuple-element.219, s32[]{:T(128)S(6)} %select_n.40, pred[46]{0:T(512)(128)(4,1)S(1)} %add_compare_fusion.2), kind=kOutput, calls=%fused_computation.2.clone.1 | convolution fusion | flops 386629632 | bytes 10551346 | tf_op jit(solution)/shard_map/while/body/eval_jaxpr/gik,gkf->gif/dot_general | solution.py:36
  75.5 14.4 %scatter_fusion = f32[32,128,256]{2,1,0:T(8,128)} fusion(f32[32,128,256]{2,1,0:T(8,128)} %get-tuple-element.205, s32[46]{0:T(128)S(1)} %get-tuple-element.191, f32[46,128,256]{2,1,0:T(8,128)} %fusion.13), kind=kCustom, calls=%fused_computation.1.clone.1 | custom fusion | flops 1507328 | bytes 18088120 | tf_op jit(solution)/shard_map/while/body/eval_jaxpr/scatter-add | solution.py:37
  89.9 0.7 add_compare_fusion.2
  90.5 0.1 compare_select_fusion.3
  90.6 2.9 gather_fusion
  93.5 5.0 %fusion.13 = f32[46,128,256]{2,1,0:T(8,128)} fusion(bf16[46,128,256]{2,1,0:T(8,128)(2,1)S(1)} %gather_fusion, bf16[368,128,128]{2,1,0:T(8,128)(2,1)} %get-tuple-element.219, s32[]{:T(128)S(6)} %select_n.40, pred[46]{0:T(512)(128)(4,1)S(1)} %add_compare_fusion.2), kind=kOutput, calls=%fused_computation.2.clone.1 | convolution fusion | flops 386629632 | bytes 10551346 | tf_op jit(solution)/shard_map/while/body/eval_jaxpr/gik,gkf->gif/dot_general | solution.py:36
  98.5 14.5 %scatter_fusion = f32[32,128,256]{2,1,0:T(8,128)} fusion(f32[32,128,256]{2,1,0:T(8,128)} %get-tuple-element.205, s32[46]{0:T(128)S(1)} %get-tuple-element.191, f32[46,128,256]{2,1,0:T(8,128)} %fusion.13), kind=kCustom, calls=%fused_computation.1.clone.1 | custom fusion | flops 1507328 | bytes 18088120 | tf_op jit(solution)/shard_map/while/body/eval_jaxpr/scatter-add | solution.py:37
  113.0 0.7 add_compare_fusion.2
  113.6 0.1 compare_select_fusion.3
  113.7 2.9 gather_fusion
  116.6 5.0 %fusion.13 = f32[46,128,256]{2,1,0:T(8,128)} fusion(bf16[46,128,256]{2,1,0:T(8,128)(2,1)S(1)} %gather_fusion, bf16[368,128,128]{2,1,0:T(8,128)(2,1)} %get-tuple-element.219, s32[]{:T(128)S(6)} %select_n.40, pred[46]{0:T(512)(128)(4,1)S(1)} %add_compare_fusion.2), kind=kOutput, calls=%fused_computation.2.clone.1 | convolution fusion | flops 386629632 | bytes 10551346 | tf_op jit(solution)/shard_map/while/body/eval_jaxpr/gik,gkf->gif/dot_general | solution.py:36
  121.6 14.5 %scatter_fusion = f32[32,128,256]{2,1,0:T(8,128)} fusion(f32[32,128,256]{2,1,0:T(8,128)} %get-tuple-element.205, s32[46]{0:T(128)S(1)} %get-tuple-element.191, f32[46,128,256]{2,1,0:T(8,128)} %fusion.13), kind=kCustom, calls=%fused_computation.1.clone.1 | custom fusion | flops 1507328 | bytes 18088120 | tf_op jit(solution)/shard_map/while/body/eval_jaxpr/scatter-add | solution.py:37
  136.1 0.7 add_compare_fusion.2
  136.7 0.1 compare_select_fusion.3
  136.8 2.9 gather_fusion
  139.8 5.0 %fusion.13 = f32[46,128,256]{2,1,0:T(8,128)} fusion(bf16[46,128,256]{2,1,0:T(8,128)(2,1)S(1)} %gather_fusion, bf16[368,128,128]{2,1,0:T(8,128)(2,1)} %get-tuple-element.219, s32[]{:T(128)S(6)} %select_n.40, pred[46]{0:T(512)(128)(4,1)S(1)} %add_compare_fusion.2), kind=kOutput, calls=%fused_computation.2.clone.1 | convolution fusion | flops 386629632 | bytes 10551346 | tf_op jit(solution)/shard_map/while/body/eval_jaxpr/gik,gkf->gif/dot_general | solution.py:36
  144.7 14.3 %scatter_fusion = f32[32,128,256]{2,1,0:T(8,128)} fusion(f32[32,128,256]{2,1,0:T(8,128)} %get-tuple-element.205, s32[46]{0:T(128)S(1)} %get-tuple-element.191, f32[46,128,256]{2,1,0:T(8,128)} %fusion.13), kind=kCustom, calls=%fused_computation.1.clone.1 | custom fusion | flops 1507328 | bytes 18088120 | tf_op jit(solution)/shard_map/while/body/eval_jaxpr/scatter-add | solution.py:37
  159.0 0.7 add_compare_fusion.2
  159.7 0.1 compare_select_fusion.3
  159.8 2.9 gather_fusion
  162.7 5.0 %fusion.13 = f32[46,128,256]{2,1,0:T(8,128)} fusion(bf16[46,128,256]{2,1,0:T(8,128)(2,1)S(1)} %gather_fusion, bf16[368,128,128]{2,1,0:T(8,128)(2,1)} %get-tuple-element.219, s32[]{:T(128)S(6)} %select_n.40, pred[46]{0:T(512)(128)(4,1)S(1)} %add_compare_fusion.2), kind=kOutput, calls=%fused_computation.2.clone.1 | convolution fusion | flops 386629632 | bytes 10551346 | tf_op jit(solution)/shard_map/while/body/eval_jaxpr/gik,gkf->gif/dot_general | solution.py:36
  167.7 14.6 %scatter_fusion = f32[32,128,256]{2,1,0:T(8,128)} fusion(f32[32,128,256]{2,1,0:T(8,128)} %get-tuple-element.205, s32[46]{0:T(128)S(1)} %get-tuple-element.191, f32[46,128,256]{2,1,0:T(8,128)} %fusion.13), kind=kCustom, calls=%fused_computation.1.clone.1 | custom fusion | flops 1507328 | bytes 18088120 | tf_op jit(solution)/shard_map/while/body/eval_jaxpr/scatter-add | solution.py:37
  182.3 0.7 add_compare_fusion.2
  182.9 0.1 compare_select_fusion.3
  183.0 2.9 gather_fusion
  186.0 5.0 %fusion.13 = f32[46,128,256]{2,1,0:T(8,128)} fusion(bf16[46,128,256]{2,1,0:T(8,128)(2,1)S(1)} %gather_fusion, bf16[368,128,128]{2,1,0:T(8,128)(2,1)} %get-tuple-element.219, s32[]{:T(128)S(6)} %select_n.40, pred[46]{0:T(512)(128)(4,1)S(1)} %add_compare_fusion.2), kind=kOutput, calls=%fused_computation.2.clone.1 | convolution fusion | flops 386629632 | bytes 10551346 | tf_op jit(solution)/shard_map/while/body/eval_jaxpr/gik,gkf->gif/dot_general | solution.py:36
  190.9 14.6 %scatter_fusion = f32[32,128,256]{2,1,0:T(8,128)} fusion(f32[32,128,256]{2,1,0:T(8,128)} %get-tuple-element.205, s32[46]{0:T(128)S(1)} %get-tuple-element.191, f32[46,128,256]{2,1,0:T(8,128)} %fusion.13), kind=kCustom, calls=%fused_computation.1.clone.1 | custom fusion | flops 1507328 | bytes 18088120 | tf_op jit(solution)/shard_map/while/body/eval_jaxpr/scatter-add | solution.py:37
  205.6 0.7 add_compare_fusion.2
  206.2 0.1 compare_select_fusion.3
  206.3 2.9 gather_fusion
  209.2 5.0 %fusion.13 = f32[46,128,256]{2,1,0:T(8,128)} fusion(bf16[46,128,256]{2,1,0:T(8,128)(2,1)S(1)} %gather_fusion, bf16[368,128,128]{2,1,0:T(8,128)(2,1)} %get-tuple-element.219, s32[]{:T(128)S(6)} %select_n.40, pred[46]{0:T(512)(128)(4,1)S(1)} %add_compare_fusion.2), kind=kOutput, calls=%fused_computation.2.clone.1 | convolution fusion | flops 386629632 | bytes 10551346 | tf_op jit(solution)/shard_map/while/body/eval_jaxpr/gik,gkf->gif/dot_general | solution.py:36
  214.2 14.6 %scatter_fusion = f32[32,128,256]{2,1,0:T(8,128)} fusion(f32[32,128,256]{2,1,0:T(8,128)} %get-tuple-element.205, s32[46]{0:T(128)S(1)} %get-tuple-element.191, f32[46,128,256]{2,1,0:T(8,128)} %fusion.13), kind=kCustom, calls=%fused_computation.1.clone.1 | custom fusion | flops 1507328 | bytes 18088120 | tf_op jit(solution)/shard_map/while/body/eval_jaxpr/scatter-add | solution.py:37
  228.8 0.7 add_compare_fusion.2
  229.5 0.1 compare_select_fusion.3
  229.6 2.9 gather_fusion
  232.5 5.0 %fusion.13 = f32[46,128,256]{2,1,0:T(8,128)} fusion(bf16[46,128,256]{2,1,0:T(8,128)(2,1)S(1)} %gather_fusion, bf16[368,128,128]{2,1,0:T(8,128)(2,1)} %get-tuple-element.219, s32[]{:T(128)S(6)} %select_n.40, pred[46]{0:T(512)(128)(4,1)S(1)} %add_compare_fusion.2), kind=kOutput, calls=%fused_computation.2.clone.1 | convolution fusion | flops 386629632 | bytes 10551346 | tf_op jit(solution)/shard_map/while/body/eval_jaxpr/gik,gkf->gif/dot_general | solution.py:36
  237.5 14.6 %scatter_fusion = f32[32,128,256]{2,1,0:T(8,128)} fusion(f32[32,128,256]{2,1,0:T(8,128)} %get-tuple-element.205, s32[46]{0:T(128)S(1)} %get-tuple-element.191, f32[46,128,256]{2,1,0:T(8,128)} %fusion.13), kind=kCustom, calls=%fused_computation.1.clone.1 | custom fusion | flops 1507328 | bytes 18088120 | tf_op jit(solution)/shard_map/while/body/eval_jaxpr/scatter-add | solution.py:37
  252.0 3.8 %convert_element_type.6 = bf16[32,128,256]{2,1,0:T(8,128)(2,1)} convert(f32[32,128,256]{2,1,0:T(8,128)} %get-tuple-element.129) | non-fusion elementwise | flops 1048576 | bytes 6291456 | tf_op jit(solution)/shard_map/convert_element_type | solution.py:43
  255.9 43.6 %reduce-scatter.2.cloned.1.call-done = bf16[1024,256]{1,0:T(8,128)(2,1)} async-done(((bf16[4096,256]{1,0:T(8,128)(2,1)}), bf16[1024,256]{1,0:T(8,128)(2,1)}) %reduce-scatter.2.cloned.1.call-update) | async-done | bytes 524304 | tf_op jit(solution)/shard_map/reduce_scatter | solution.py:42
  (15 shorter events, 0.1 us)
Async XLA Ops:
  9.8 5.4 %copy-start = (s32[1,1,368]{2,1,0:T(1,128)S(1)}, s32[1,1,368]{2,1,0:T(1,128)}, u32[]{:S(2)}) copy-start(s32[1,1,368]{2,1,0:T(1,128)} %param.8) | copy-start | bytes 4420
  9.8 5.4 %copy-start.1 = (s32[1,1,368]{2,1,0:T(1,128)S(1)}, s32[1,1,368]{2,1,0:T(1,128)}, u32[]{:S(2)}) copy-start(s32[1,1,368]{2,1,0:T(1,128)} %param.9) | copy-start | bytes 4420
  9.8 54.5 %all-to-all-start = ((bf16[8,1024,256]{2,1,0:T(8,128)(2,1)}), bf16[8,1024,256]{2,1,0:T(8,128)(2,1)}, u32[]{:S(2)}, u32[]{:S(2)}) async-start(bf16[8,1024,256]{2,1,0:T(8,128)(2,1)} %stack.2), calls=%async_computation | async-start | bytes 8388608 | tf_op jit(solution)/shard_map/all_to_all | solution.py:18
  15.1 284.4 %reduce-scatter.2.cloned.1.call-start = ((), (), s32[]{:S(2)}) async-start(), calls=%async_computation.2 | async-start | bytes 2621440 | tf_op jit(solution)/shard_map/reduce_scatter | solution.py:42
Sparse Core Ops, SparseCore 0:
  256.0 43.4 reduce-scatter.1
